TPU v7x, 32 devices: a whole 2x2x4 slice. The times are simulated.
32 devices in a mesh: gx: 4 (over x, core), gy: 2 (over y), gz: 4 (over z).
Axes of the slice: x: 2, y: 2, z: 4, core: 2. Of those that a mesh axis runs over, the one named last changes fastest.
Arguments:
- velocity: float32 [3, 128, 192, 1024], P(None, 'gx', 'gy', 'gz'), may hold values from -6 to 6
Outputs:
- magnitude: float32 [128, 192, 1024], P('gx', ('gy', 'gz'))
- level_one: float32 [64, 96, 512], P('gx', 'gy')
- level_two: float32 [32, 48, 256], P('gx', 'gy')
- level_three: float32 [16, 24, 128], P('gx', 'gy')
- level_four: float32 [8, 12, 64], P('gx', 'gy')
- level_five: float32 [4, 6, 32], P('gx', 'gy')
All inputs are finite; a program needn't handle non-finite values.
Results may differ from a plain program's by a relative error of at most 0.000075.
Values sent between devices are 32-bit elements; how exact they have to be, the bound alone decides.
A program may use at most 256 MiB of HBM per device.

v0:
```python
import jax
import jax.numpy as jnp
from jax import lax
from jax.sharding import PartitionSpec as P


def extended(value, sides, width):
    for axis, dim in sides:
        peers, length = (lax.axis_size(axis), value.shape[dim])
        up = [(i, (i + 1) % peers) for i in range(peers)]
        down = [(j, i) for i, j in up]
        last = lax.slice_in_dim(value, length - width, length, axis=dim)
        leading = lax.slice_in_dim(value, 0, width, axis=dim)
        before = lax.ppermute(last, axis, up)
        after = lax.ppermute(leading, axis, down)
        value = jnp.concatenate([before, value, after], axis=dim)
    return value


def depth_diff(field, before, after):
    ahead = jnp.roll(field, -1, 2)
    behind = jnp.roll(field, 1, 2)
    depth_index = lax.broadcasted_iota(jnp.int32, field.shape, 2)
    ahead = jnp.where(depth_index == field.shape[2] - 1, after[:, :, None], ahead)
    behind = jnp.where(depth_index == 0, before[:, :, None], behind)
    return (ahead - behind) * 0.5


def vorticity(padded, before, after):
    inner = padded[:, 1:-1, 1:-1, :]

    def first_diff(comp):
        return (padded[comp, 2:, 1:-1, :] - padded[comp, :-2, 1:-1, :]) * 0.5

    def second_diff(comp):
        return (padded[comp, 1:-1, 2:, :] - padded[comp, 1:-1, :-2, :]) * 0.5

    def third_diff(comp):
        return depth_diff(inner[comp], before[comp], after[comp])

    curl_first = second_diff(2) - third_diff(1)
    curl_second = third_diff(0) - first_diff(2)
    curl_third = first_diff(1) - second_diff(0)
    return jnp.sqrt(
        1.0 + curl_first * curl_first + curl_second * curl_second + curl_third * curl_third
    )


def pooled(field):
    rows, cols, depth = field.shape
    summed = field.reshape(rows // 2, 2, cols, depth).sum(axis=1)
    summed = summed.reshape(rows // 2, cols // 2, 2, depth).sum(axis=2)
    pairing = (
        lax.broadcasted_iota(jnp.int32, (depth, depth // 2), 0) // 2
        == lax.broadcasted_iota(jnp.int32, (depth, depth // 2), 1)
    ).astype(jnp.float32)
    merged = jnp.dot(
        summed.reshape(-1, depth),
        pairing,
        precision=lax.Precision.HIGHEST,
        preferred_element_type=jnp.float32,
    )
    return merged.reshape(rows // 2, cols // 2, depth // 2) * 0.125


def end_planes(velocity):
    return jnp.concatenate([velocity[..., :1], velocity[..., -1:]], axis=3)


def on_device(velocity):
    padded = extended(velocity, (("gx", 1), ("gy", 2)), 1)
    planes = extended(end_planes(velocity), (("gz", 3),), 1)
    block_mag = vorticity(padded, planes[..., 0], planes[..., 3])
    pencil = lax.all_to_all(block_mag, "gz", split_axis=1, concat_axis=2, tiled=True)
    level_one = lax.all_gather(pooled(pencil), "gz", axis=1, tiled=True)
    level_two = pooled(level_one)
    level_three = pooled(level_two)
    level_four = pooled(level_three)
    level_five = pooled(level_four)
    return (pencil, level_one, level_two, level_three, level_four, level_five)


def solution(mesh):
    in_specs = (P(None, "gx", "gy", "gz"),)
    out_specs = (
        P("gx", ("gy", "gz"), None),
        P("gx", "gy", None),
        P("gx", "gy", None),
        P("gx", "gy", None),
        P("gx", "gy", None),
        P("gx", "gy", None),
    )
    return jax.shard_map(
        on_device, mesh=mesh, in_specs=in_specs, out_specs=out_specs, check_vma=False
    )
```

profile of v0, /device:TPU:0, one launch (start us, length us, event | category | flops | bytes accessed | tf_op | source)
XLA Modules:
  0.0 252.0 jit_solution(13280708438288536689)
XLA Ops:
  9.3 2.4 collective-permute-start.1
  12.8 8.7 %fusion.60 = (f32[3,32,96,1]{3,2,1,0:T(8,128)}, f32[3,32,96,1]{3,2,1,0:T(8,128)}) fusion(f32[3,32,96,256]{3,2,1,0:T(8,128)} %param.1), kind=kLoop, calls=%fused_computation.114 | loop fusion | bytes 147456 | tf_op jit(solution)/shard_map/slice | solution.py:67
  21.5 3.1 %copy.129 = f32[3,32,96,1]{2,1,3,0:T(8,128)S(1)} copy(f32[3,32,96,1]{3,2,1,0:T(8,128)} %get-tuple-element.51) | data formatting | bytes 73728
  24.6 1.6 collective-permute-start.5
  26.2 3.1 %copy.128 = f32[3,32,96,1]{2,1,3,0:T(8,128)S(1)} copy(f32[3,32,96,1]{3,2,1,0:T(8,128)} %get-tuple-element.50) | data formatting | bytes 73728
  29.3 2.5 collective-permute-start.4
  31.8 16.0 %constant_dynamic-update-slice_fusion = (f32[3,33,96,256]{3,1,2,0:T(8,128)}, f32[3,32,96,256]{3,1,2,0:T(8,128)}) fusion(f32[3,32,96,256]{3,2,1,0:T(8,128)} %param.1), kind=kLoop, calls=%fused_computation.93 | loop fusion | bytes 28311552
  47.7 3.6 %slice_bitcast_fusion = (f32[32,96,256]{2,0,1:T(8,128)S(1)}, f32[32,96,256]{2,0,1:T(8,128)S(1)}) fusion(f32[3,32,96,256]{3,1,2,0:T(8,128)} %get-tuple-element.55), kind=kLoop, calls=%fused_computation.22 | loop fusion | bytes 12582912 | tf_op jit(solution)/shard_map/squeeze | solution.py:39
  51.3 3.7 %fusion.62 = (f32[32,96,1]{2,0,1:T(8,128)}, f32[32,96,1]{2,0,1:T(8,128)}, f32[32,96,1]{2,0,1:T(8,128)}, f32[32,96,1]{2,0,1:T(8,128)}) fusion(f32[32,96,256]{2,0,1:T(8,128)S(1)} %get-tuple-element.52, f32[32,96,256]{2,0,1:T(8,128)S(1)} %get-tuple-element.53), kind=kLoop, calls=%fused_computation.116 | loop fusion | bytes 98304 | tf_op jit(solution)/shard_map/jit(_roll_static)/slice | solution.py:22
  55.0 6.5 %fusion.63 = (f32[32,96,255]{2,0,1:T(8,128)}, f32[32,96,255]{2,0,1:T(8,128)}, f32[32,96,255]{2,0,1:T(8,128)}, f32[32,96,255]{2,0,1:T(8,128)}) fusion(f32[32,96,256]{2,0,1:T(8,128)S(1)} %get-tuple-element.52, f32[32,96,256]{2,0,1:T(8,128)S(1)} %get-tuple-element.53), kind=kLoop, calls=%fused_computation.117 | loop fusion | bytes 25067520 | tf_op jit(solution)/shard_map/jit(_roll_static)/slice | solution.py:22
  62.8 1.8 pad_maximum_fusion.9
  64.7 1.5 collective-permute-start.2
  66.7 1.3 slice_bitcast_fusion.5
  68.2 1.4 copy.106
  69.6 1.4 copy.110
  71.1 7.8 %dynamic-update-slice.1 = f32[3,33,96,256]{3,1,2,0:T(8,128)} dynamic-update-slice(f32[3,33,96,256]{3,1,2,0:T(8,128)} %get-tuple-element.54, f32[3,1,96,256]{3,1,2,0:T(1,128)S(1)} %collective-permute-done.1, s32[]{} %constant.86, s32[]{} %constant.87, s32[]{} %constant.86, s32[]{} %constant.86) | dynamic-update-slice | bytes 589828 | tf_op jit(solution)/shard_map/concatenate | solution.py:16
  78.9 21.6 %fusion.6 = f32[32,96,256]{2,0,1:T(8,128)} fusion(f32[3,34,1,256]{3,1,2,0:T(8,128)} %collective-permute-done.3, f32[3,1,96,256]{3,1,2,0:T(1,128)S(1)} %collective-permute-done.1, f32[3,32,96,256]{3,1,2,0:T(8,128)} %get-tuple-element.55, f32[3,1,96,256]{3,1,2,0:T(1,128)} %collective-permute-done, f32[3,34,1,256]{3,1,2,0:T(8,128)} %collective-permute-done.2, ...), kind=kLoop, calls=%fused_computation.7 | loop fusion | flops 33816576 | bytes 32305664 | tf_op jit(solution)/shard_map/sqrt | solution.py:44
  100.5 3.7 %all-to-all-start = ((f32[32,96,256]{2,0,1:T(8,128)}), f32[32,96,256]{2,0,1:T(8,128)S(1)}, u32[]{:S(2)}, u32[]{:S(2)}) async-start(f32[32,96,256]{2,0,1:T(8,128)} %fusion.6), calls=%async_computation | async-start | bytes 6291456 | tf_op jit(solution)/shard_map/all_to_all | solution.py:74
  104.3 70.6 %all-to-all-done = f32[32,96,256]{2,0,1:T(8,128)S(1)} async-done(((f32[32,96,256]{2,0,1:T(8,128)}), f32[32,96,256]{2,0,1:T(8,128)S(1)}, u32[]{:S(2)}, u32[]{:S(2)}) %all-to-all-start) | async-done | bytes 3145760 | tf_op jit(solution)/shard_map/all_to_all | solution.py:74
  175.0 1.7 copy-done.1
  176.6 3.9 %copy.145 = f32[32,4,24,256]{3,1,2,0:T(4,128)S(1)} copy(f32[32,4,24,256]{3,0,2,1:T(8,128)} %bitcast.78) | data formatting | bytes 6291456 | tf_op jit(solution)/shard_map/all_to_all | solution.py:74
  180.5 3.3 %reshape.90 = f32[16,2,24,1024]{3,2,1,0:T(8,128)} reshape(f32[32,24,4,256]{3,2,1,0:T(4,128)S(1)} %bitcast.76) | data formatting | bytes 6291456 | tf_op jit(solution)/shard_map/reshape | solution.py:51
  183.8 3.5 %reduce_sum.90 = f32[16,24,1024]{2,1,0:T(8,128)} reduce(f32[16,2,24,1024]{3,2,1,0:T(8,128)} %reshape.90, f32[]{:T(128)} %constant.81.clone.1), dimensions={1}, to_apply=%region_0.1 | reduce | flops 393216 | bytes 4718596 | tf_op jit(solution)/shard_map/reduce_sum | solution.py:51
  187.3 3.5 %copy.126 = f32[16,24,1024]{2,0,1:T(8,128)} copy(f32[16,24,1024]{2,1,0:T(8,128)} %reduce_sum.90) | data formatting | bytes 3145728 | tf_op jit(solution)/shard_map/reshape | solution.py:52
  190.8 2.5 reduce_sum.91
  193.2 3.0 %fusion.26 = f32[16,12,512]{2,0,1:T(8,128)} fusion(f32[16,12,1024]{2,0,1:T(8,128)} %reduce_sum.91, s32[1024]{0:T(1024)S(1)} %get-tuple-element.82, s32[1024]{0:T(1024)S(1)} %get-tuple-element.83, pred[1024]{0:T(1024)(128)(4,1)S(1)} %fusion.56), kind=kOutput, calls=%fused_computation.42 | convolution fusion | flops 1209106432 | bytes 1188864 | tf_op jit(solution)/shard_map/dot_general | solution.py:57
  196.4 3.0 %all_to_all.16 = f32[32,24,1024]{2,1,0:T(8,128)} reshape(f32[32,24,4,256]{3,2,1,0:T(4,128)S(1)} %bitcast.77) | data formatting | bytes 6291456 | tf_op jit(solution)/shard_map/all_to_all | solution.py:74
  199.4 33.1 %all-gather.2.cloned.1.call-done = f32[16,48,512]{2,0,1:T(8,128)} async-done(((f32[16,12,512]{2,0,1:T(8,128)}), f32[16,48,512]{2,0,1:T(8,128)}) %all-gather.2.cloned.1.call-update) | async-done | bytes 1572880 | tf_op jit(solution)/shard_map/all_gather | solution.py:75
  232.6 2.2 reshape.92
  234.8 3.0 %reduce_sum.92 = f32[8,48,512]{2,0,1:T(8,128)} reduce(f32[8,2,48,512]{3,1,0,2:T(2,128)S(1)} %reshape.92, f32[]{:T(128)} %constant.81.clone.1), dimensions={1}, to_apply=%region_2.3 | reduce | flops 196608 | bytes 2359300 | tf_op jit(solution)/shard_map/reduce_sum | solution.py:51
  239.0 1.4 bitcast_reduce_fusion
  243.1 2.1 copy.122
  (45 shorter events, 9.1 us)
Async XLA Ops:
  9.3 53.5 %collective-permute-start.1 = (f32[3,1,96,256]{3,1,2,0:T(1,128)}, f32[3,1,96,256]{3,1,2,0:T(1,128)S(1)}, u32[]{:S(2)}, u32[]{:S(2)}) collective-permute-start(f32[3,1,96,256]{3,1,2,0:T(1,128)} %copy.103), channel_id=1, source_target_pairs={{8,0},{16,8},{24,16},{0,24},{9,1},{17,9},{25,17},{1,25},{10,2},{18... | collective-permute-start | bytes 884744 | tf_op jit(solution)/shard_map/ppermute | solution.py:15
  12.8 50.1 %collective-permute-start = (f32[3,1,96,256]{3,1,2,0:T(1,128)}, f32[3,1,96,256]{3,1,2,0:T(1,128)}, u32[]{:S(2)}, u32[]{:S(2)}) collective-permute-start(f32[3,1,96,256]{3,1,2,0:T(1,128)} %copy.102), channel_id=1, source_target_pairs={{0,8},{8,16},{16,24},{24,0},{1,9},{9,17},{17,25},{25,1},{2,10},{10... | collective-permute-start | bytes 884744 | tf_op jit(solution)/shard_map/ppermute | solution.py:14
  24.6 37.5 %collective-permute-start.5 = (f32[3,32,96,1]{2,1,3,0:T(8,128)S(1)}, f32[3,32,96,1]{2,1,3,0:T(8,128)}, u32[]{:S(2)}, u32[]{:S(2)}) collective-permute-start(f32[3,32,96,1]{2,1,3,0:T(8,128)S(1)} %copy.129), channel_id=1, source_target_pairs={{0,1},{1,2},{2,3},{3,0},{4,5},{5,6},{6,7},{7,4},{8,9},{9,10},{10,1... | collective-permute-start | bytes 110600 | tf_op jit(solution)/shard_map/ppermute | solution.py:14
  29.3 37.4 %collective-permute-start.4 = (f32[3,32,96,1]{2,1,3,0:T(8,128)S(1)}, f32[3,32,96,1]{2,1,3,0:T(8,128)}, u32[]{:S(2)}, u32[]{:S(2)}) collective-permute-start(f32[3,32,96,1]{2,1,3,0:T(8,128)S(1)} %copy.128), channel_id=1, source_target_pairs={{1,0},{2,1},{3,2},{0,3},{5,4},{6,5},{7,6},{4,7},{9,8},{10,9},{11,1... | collective-permute-start | bytes 110600 | tf_op jit(solution)/shard_map/ppermute | solution.py:15
  62.8 16.1 %copy-start = (f32[32,96,255]{2,0,1:T(8,128)S(1)}, f32[32,96,255]{2,0,1:T(8,128)}, u32[]{:S(2)}) copy-start(f32[32,96,255]{2,0,1:T(8,128)} %get-tuple-element.60) | copy-start | bytes 9400324
  64.7 14.2 %collective-permute-start.2 = (f32[3,34,1,256]{3,1,2,0:T(8,128)}, f32[3,34,1,256]{3,1,2,0:T(8,128)}, u32[]{:S(2)}, u32[]{:S(2)}) collective-permute-start(f32[3,34,1,256]{3,1,2,0:T(8,128)} %get-tuple-element.48), channel_id=1, source_target_pairs={{4,0},{0,4},{5,1},{1,5},{6,2},{2,6},{7,3},{3,7},{12,8},{8,12},{13,... | collective-permute-start | bytes 313352 | tf_op jit(solution)/shard_map/ppermute | solution.py:15
  66.2 12.7 %collective-permute-start.3 = (f32[3,34,1,256]{3,1,2,0:T(8,128)}, f32[3,34,1,256]{3,1,2,0:T(8,128)}, u32[]{:S(2)}, u32[]{:S(2)}) collective-permute-start(f32[3,34,1,256]{3,1,2,0:T(8,128)} %get-tuple-element.49), channel_id=1, source_target_pairs={{0,4},{4,0},{1,5},{5,1},{2,6},{6,2},{3,7},{7,3},{8,12},{12,8},{9,1... | collective-permute-start | bytes 313352 | tf_op jit(solution)/shard_map/ppermute | solution.py:14
  100.5 74.4 %all-to-all-start = ((f32[32,96,256]{2,0,1:T(8,128)}), f32[32,96,256]{2,0,1:T(8,128)S(1)}, u32[]{:S(2)}, u32[]{:S(2)}) async-start(f32[32,96,256]{2,0,1:T(8,128)} %fusion.6), calls=%async_computation | async-start | bytes 6291456 | tf_op jit(solution)/shard_map/all_to_all | solution.py:74
  104.2 128.3 %all-gather.2.cloned.1.call-start = ((), (), s32[]{:S(2)}) async-start(), calls=%async_computation.1 | async-start | bytes 1966080 | tf_op jit(solution)/shard_map/all_gather | solution.py:75
  175.0 1.7 copy-start.1
  234.8 8.3 %copy-start.2 = (f32[16,48,512]{2,0,1:T(8,128)S(1)}, f32[16,48,512]{2,0,1:T(8,128)}, u32[]{:S(2)}) copy-start(f32[16,48,512]{2,0,1:T(8,128)} %all-gather.2.cloned.1.call-done) | copy-start | bytes 4718596
Sparse Core Ops, SparseCore 0:
  196.4 36.0 all-gather.1
where the time goes:
time: 253 us; the launch traced here: 252 us
  waiting for transfers between devices  104 us (41%)
  local copies, waits for them, and re-layouts  82.3 us (33%)
  other arithmetic  34.2 us (14%)
  between operations  14.2 us (6%)
  starting transfers between devices  12.3 us (5%)
  matrix products  5.12 us (2%)
    all_to_all x1, waiting for transfers between devices, on_device(): lax.all_to_all(block_mag, 'gz', split_axis=1, concat_axis=2, tiled=True)  70.6 us
    all_gather x1, waiting for transfers between devices, on_device(): level_one = lax.all_gather(pooled(pencil), 'gz', axis=1, tiled=True)  33.1 us
    unnamed x13, local copies, waits for them, and re-layouts  27.7 us
    sqrt x1, other arithmetic, vorticity(): jnp.sqrt(1.0 + curl_first * curl_first + curl_second * curl_second + curl...  21.6 us
    slice x2, local copies, waits for them, and re-layouts, depth_diff(): behind = jnp.roll(field, 1, 2)  10.2 us
    slice x1, local copies, waits for them, and re-layouts, end_planes(): return jnp.concatenate([velocity[..., :1], velocity[..., -1:]], axis=3)  8.69 us
    concatenate x1, local copies, waits for them, and re-layouts, extended(): value = jnp.concatenate([before, value, after], axis=dim)  7.82 us
    all_to_all x2, local copies, waits for them, and re-layouts, on_device(): lax.all_to_all(block_mag, 'gz', split_axis=1, concat_axis=2, tiled=True)  6.95 us
  transfers between devices with their start and end apart: 8, of which 2 were waited for; matrix products, arithmetic and copies ran while one was open for 24% of the time, Pallas kernels for 0%

commit v1 on v0

v1 whole, which is shorter than its diff:
```python
import functools

import jax
import jax.numpy as jnp
from jax import lax
from jax.experimental import pallas as pl
from jax.experimental.pallas import tpu as pltpu
from jax.sharding import PartitionSpec as P

MESH = pl.DeviceIdType.MESH
LANES = 128
LOADS = 4


def remote(src, dst, send, recv, device):
    return pltpu.make_async_remote_copy(
        src_ref=src, dst_ref=dst, send_sem=send, recv_sem=recv, device_id=device, device_id_type=MESH
    )


def halves(size, along):
    shape = (size, size // 2) if along else (size // 2, size)
    fine = lax.broadcasted_iota(jnp.int32, shape, 1 - along)
    coarse = lax.broadcasted_iota(jnp.int32, shape, along)
    return jnp.where(fine // 2 == coarse, 1.0, 0.0).astype(jnp.float32)


def dot(a, b):
    return jnp.dot(a, b, precision=lax.Precision.HIGHEST, preferred_element_type=jnp.float32)


def merge(summed):
    rows, depth = summed.shape
    across = dot(summed, halves(depth, 1))
    return dot(halves(rows, 0), across) * 0.125


def kernel(
    sizes, vel_hbm, pencil, one_out, two, three, four, five,
    vel, ypack, yhalo, zpack, zhalo, stage, one, own_one,
    load_sem, xs_sem, xr_sem, ys_sem, yr_sem, zs_sem, zr_sem,
    as_sem, ar_sem, own_sem, up_sem, down_sem, one_sem, store_sem,
):
    nx, ny, nz = sizes
    gx, gy, me = lax.axis_index("gx"), lax.axis_index("gy"), lax.axis_index("gz")
    _, planes, cols, depth = vel_hbm.shape
    rows = cols // nz
    half = depth // 2

    def at(dx=0, dy=0, dz=0):
        return (lax.rem(gx + dx + nx, nx), lax.rem(gy + dy + ny, ny), lax.rem(me + dz + nz, nz))

    barrier = pltpu.get_barrier_semaphore()
    friends = [at(dx=1), at(dx=-1), at(dy=1), at(dy=-1)] + [at(dz=d) for d in range(1, nz)]
    for friend in friends:
        pl.semaphore_signal(barrier, inc=1, device_id=friend, device_id_type=MESH)

    step = planes // LOADS
    loads = []
    for k in range(LOADS):
        loads.append(pltpu.make_async_copy(
            vel_hbm.at[:, pl.ds(k * step, step)], vel.at[:, pl.ds(1 + k * step, step)], load_sem.at[k]))
        loads[-1].start()
    pl.semaphore_wait(barrier, len(friends))

    xcopies = [
        remote(vel_hbm.at[pl.ds(1, 2), planes - 1], vel.at[pl.ds(1, 2), 0], xs_sem.at[0], xr_sem.at[0], at(dx=1)),
        remote(vel_hbm.at[pl.ds(1, 2), 0], vel.at[pl.ds(1, 2), planes + 1], xs_sem.at[1], xr_sem.at[1], at(dx=-1)),
    ]
    for copy in xcopies:
        copy.start()

    lane = lax.broadcasted_iota(jnp.int32, (cols, LANES), 1)

    def pack(x, carry):
        first, last = carry
        for c in range(2):
            first = jnp.where(lane == c * planes + x, vel[c, x + 1, :, 0:1], first)
            last = jnp.where(lane == c * planes + x, vel[c, x + 1, :, depth - 1:depth], last)
            ypack[0, c, pl.ds(x, 1), :] = vel[2 * c, x + 1, 0:1, :]
            ypack[1, c, pl.ds(x, 1), :] = vel[2 * c, x + 1, cols - 1:cols, :]
        return first, last

    carry = (jnp.zeros((cols, LANES), jnp.float32), jnp.zeros((cols, LANES), jnp.float32))
    for k in range(LOADS):
        loads[k].wait()
        carry = lax.fori_loop(k * step, (k + 1) * step, pack, carry)
    zpack[0], zpack[1] = carry
    side = [
        remote(ypack.at[1], yhalo.at[0], ys_sem.at[0], yr_sem.at[0], at(dy=1)),
        remote(ypack.at[0], yhalo.at[1], ys_sem.at[1], yr_sem.at[1], at(dy=-1)),
        remote(zpack.at[1], zhalo.at[0], zs_sem.at[0], zr_sem.at[0], at(dz=1)),
        remote(zpack.at[0], zhalo.at[1], zs_sem.at[1], zr_sem.at[1], at(dz=-1)),
    ]
    for copy in side:
        copy.start()
    for copy in xcopies + side:
        copy.wait_recv()

    row = lax.broadcasted_iota(jnp.int32, (cols, depth), 0)
    deep = lax.broadcasted_iota(jnp.int32, (cols, depth), 1)

    def second(c, x):
        field = vel[2 * c, x + 1]
        ahead = jnp.where(row == cols - 1, yhalo[1, c, pl.ds(x, 1), :], pltpu.roll(field, cols - 1, 0))
        behind = jnp.where(row == 0, yhalo[0, c, pl.ds(x, 1), :], pltpu.roll(field, 1, 0))
        return ahead - behind

    def third(c, x):
        field = vel[c, x + 1]
        shift = LANES - (c * planes + x)
        shift = jnp.where(shift == LANES, 0, shift)
        after = pltpu.roll(zhalo[1], shift, 1)[:, 0:1]
        before = pltpu.roll(zhalo[0], shift, 1)[:, 0:1]
        ahead = jnp.where(deep == depth - 1, after, pltpu.roll(field, depth - 1, 1))
        behind = jnp.where(deep == 0, before, pltpu.roll(field, 1, 1))
        return ahead - behind

    def magnitude(x):
        total = second(1, x) - third(1, x)
        total = total * total
        part = third(0, x) - (vel[2, x + 2] - vel[2, x])
        total = total + part * part
        part = (vel[1, x + 2] - vel[1, x]) - second(0, x)
        total = total + part * part
        return jnp.sqrt(1.0 + 0.25 * total)

    def block(target, first, count):
        here = pl.ds(pl.multiple_of(me * depth, LANES), depth)
        return remote(
            stage.at[target, pl.ds(first, count)], pencil.at[pl.ds(first, count), :, here],
            as_sem.at[target], ar_sem.at[me], (gx, gy, target))

    def near(first):
        @pl.when(me < nz - 1)
        def _():
            block(me + 1, first, 2).start()

        @pl.when(me > 0)
        def _():
            block(me - 1, first, 2).start()

    def pair(i, carry):
        x = 2 * i
        summed = None
        for k in range(2):
            value = magnitude(x + k)
            for q in range(nz):
                stage[q, x + k] = value[q * rows:(q + 1) * rows, :]
            summed = value if summed is None else summed + value

        @pl.when(i > 0)
        def _():
            near(x - 2)
        own_one[i] = merge(summed)
        return carry

    lax.fori_loop(0, planes // 2, pair, 0)
    near(planes - 2)

    def lanes_of(piece):
        return one.at[:, :, pl.ds(pl.multiple_of(piece * half, LANES), half)]

    def hop(piece, source, up):
        return remote(
            source, lanes_of(piece), (up_sem if up else down_sem).at[piece], one_sem.at[piece],
            (gx, gy, jnp.minimum(me + 1, nz - 1) if up else jnp.maximum(me - 1, 0)))

    @pl.when(me < nz - 1)
    def _():
        hop(me, own_one, True).start()

    @pl.when(me > 0)
    def _():
        hop(me, own_one, False).start()

    def far():
        for d in range(2, nz):
            @pl.when(me + d < nz)
            def _():
                block(me + d, 0, planes).start()

            @pl.when(me - d >= 0)
            def _():
                block(me - d, 0, planes).start()

    end = jnp.logical_or(me == 0, me == nz - 1)

    @pl.when(end)
    def _():
        far()
    keep = pltpu.make_async_copy(
        stage.at[me], pencil.at[:, :, pl.ds(pl.multiple_of(me * depth, LANES), depth)], own_sem.at[0])
    keep.start()
    mine = pltpu.make_async_copy(own_one, lanes_of(me), own_sem.at[1])
    mine.start()

    for k in range(1, nz):
        @pl.when(me - k >= 0)
        def _():
            hop(me - k, own_one, True).wait_recv()

            @pl.when(me < nz - 1)
            def _():
                hop(me - k, lanes_of(me - k), True).start()

        @pl.when(me + k < nz)
        def _():
            hop(me + k, own_one, False).wait_recv()

            @pl.when(me > 0)
            def _():
                hop(me + k, lanes_of(me + k), False).start()
        if k == 1:
            @pl.when(jnp.logical_not(end))
            def _():
                far()
    mine.wait()

    store = pltpu.make_async_copy(one, one_out, store_sem)
    store.start()

    def second_level(i, carry):
        two[i] = merge(one[2 * i] + one[2 * i + 1])
        return carry

    lax.fori_loop(0, two.shape[0], second_level, 0)
    for fine, coarse in ((two, three), (three, four), (four, five)):
        for i in range(coarse.shape[0]):
            coarse[i] = merge(fine[2 * i] + fine[2 * i + 1])
    store.wait()
    keep.wait()
    for copy in xcopies + side:
        copy.wait_send()
    for p in range(nz):
        @pl.when(jnp.logical_and(p <= me, me < nz - 1))
        def _():
            hop(p, own_one, True).wait_send()

        @pl.when(jnp.logical_and(p >= me, me > 0))
        def _():
            hop(p, own_one, False).wait_send()
    for p in range(nz):
        @pl.when(p != me)
        def _():
            block(p, 0, planes).wait_send()
            there = pl.ds(p * depth, depth)
            remote(stage.at[p], pencil.at[:, :, there], as_sem.at[p], ar_sem.at[p], (gx, gy, p)).wait_recv()


def on_device(velocity):
    nx, ny, nz = (lax.axis_size(a) for a in ("gx", "gy", "gz"))
    _, planes, cols, depth = velocity.shape
    full = depth * nz
    f32 = jnp.float32

    def level(k):
        return jax.ShapeDtypeStruct((planes >> k, cols >> k, full >> k), f32)

    vmem = pl.BlockSpec(memory_space=pltpu.VMEM)
    anywhere = pl.BlockSpec(memory_space=pl.ANY)
    dma = pltpu.SemaphoreType.DMA
    return pl.pallas_call(
        functools.partial(kernel, (nx, ny, nz)),
        out_shape=(jax.ShapeDtypeStruct((planes, cols // nz, full), f32),) + tuple(level(k) for k in range(1, 6)),
        in_specs=[anywhere],
        out_specs=(anywhere, anywhere, vmem, vmem, vmem, vmem),
        scratch_shapes=[
            pltpu.VMEM((3, planes + 2, cols, depth), f32),
            pltpu.VMEM((2, 2, planes, depth), f32),
            pltpu.VMEM((2, 2, planes, depth), f32),
            pltpu.VMEM((2, cols, LANES), f32),
            pltpu.VMEM((2, cols, LANES), f32),
            pltpu.VMEM((nz, planes, cols // nz, depth), f32),
            pltpu.VMEM((planes // 2, cols // 2, full // 2), f32),
            pltpu.VMEM((planes // 2, cols // 2, depth // 2), f32),
            dma((LOADS,)), dma((2,)), dma((2,)), dma((2,)), dma((2,)), dma((2,)), dma((2,)),
            dma((nz,)), dma((nz,)), dma((2,)), dma((nz,)), dma((nz,)), dma((nz,)), dma,
        ],
        compiler_params=pltpu.CompilerParams(
            collective_id=0, has_side_effects=True, vmem_limit_bytes=60 * 1024 * 1024
        ),
    )(velocity)


def solution(mesh):
    in_specs = (P(None, "gx", "gy", "gz"),)
    out_specs = (
        P("gx", ("gy", "gz"), None),
        P("gx", "gy", None),
        P("gx", "gy", None),
        P("gx", "gy", None),
        P("gx", "gy", None),
        P("gx", "gy", None),
    )
    return jax.shard_map(
        on_device, mesh=mesh, in_specs=in_specs, out_specs=out_specs, check_vma=False
    )
```

time: 253 us -> 129 us (0.51)
  Pallas kernels: 0 us -> 118 us
  waiting for transfers between devices: 104 us -> 0 us
  local copies, waits for them, and re-layouts: 82.3 us -> 9.83 us
  other arithmetic: 34.2 us -> 0 us
  between operations: 14.2 us -> 0.64 us
  starting transfers between devices: 12.3 us -> 0 us
  matrix products: 5.12 us -> 0 us
    pallas_call x0 -> x1, Pallas kernels: none -> 118 us  [on_device(): pl.pallas_call(functools.partial(kernel, (nx, ny, nz)), out_shape=(jax.Sh...]
    all_to_all x1 -> x0, waiting for transfers between devices: 70.6 us -> none  [on_device(): lax.all_to_all(block_mag, 'gz', split_axis=1, concat_axis=2, tiled=True)]
    all_gather x1 -> x0, waiting for transfers between devices: 33.1 us -> none  [on_device(): level_one = lax.all_gather(pooled(pencil), 'gz', axis=1, tiled=True)]
    slice x6 -> x0, local copies, waits for them, and re-layouts: 22.1 us -> none  [the longest x2 10.2 us: depth_diff(): behind = jnp.roll(field, 1, 2)]
    unnamed x13 -> x7, local copies, waits for them, and re-layouts: 27.7 us -> 5.91 us
    sqrt x1 -> x0, other arithmetic: 21.6 us -> none  [vorticity(): jnp.sqrt(1.0 + curl_first * curl_first + curl_second * curl_second + curl...]
    reduce_sum x7 -> x0, other arithmetic: 10.2 us -> none  [the longest x2 6.46 us: pooled(): summed = field.reshape(rows // 2, 2, cols, depth).sum(axis=1)]
    reshape x5 -> x0, local copies, waits for them, and re-layouts: 9.03 us -> none  [the longest x2 5.52 us: pooled(): summed = field.reshape(rows // 2, 2, cols, depth).sum(axis=1)]
  transfers between devices with their start and end apart: 8 -> 0, of which waited for: 2 -> 0; matrix products, arithmetic and copies ran while one was open for 24% -> 0% of each run, Pallas kernels for 0% -> 0%
where the time goes in v1:
time: 129 us
  Pallas kernels  118 us (91%)
  local copies, waits for them, and re-layouts  9.83 us (8%)
    pallas_call x1, Pallas kernels, on_device(): pl.pallas_call(functools.partial(kernel, (nx, ny, nz)), out_shape=(jax.Sh...  118 us
    unnamed x7, local copies, waits for them, and re-layouts  5.91 us
    pallas_call x3, local copies, waits for them, and re-layouts, on_device(): pl.pallas_call(functools.partial(kernel, (nx, ny, nz)), out_shape=(jax.Sh...  3.92 us

profile of v1, /device:TPU:0, one launch (start us, length us, event | category | flops | bytes accessed | tf_op | source)
XLA Modules:
  0.0 128.9 jit_solution(1939918694344882216)
XLA Ops:
  0.6 118.5 %shard_map.62 = (f32[32,24,1024]{2,1,0:T(8,128)}, f32[16,48,512]{2,1,0:T(8,128)}, f32[8,24,256]{2,1,0:T(8,128)}, f32[4,12,128]{2,1,0:T(8,128)}, f32[2,6,64]{2,1,0:T(8,128)}, /*index=5*/f32[1,3,32]{2,1,0:T(4,128)}) custom-call(f32[3,32,96,256]{3,2,1,0:T(8,128)} %vel_hbm.1), custom_call_target="tpu_custom_call" | custom-call | tf_op jit(solution)/shard_map/pallas_call | solution.py:263
  119.1 1.2 copy.9
  120.4 1.3 %copy.8 = f32[2,6,64]{2,0,1:T(2,128)} copy(f32[2,6,64]{2,1,0:T(8,128)} %get-tuple-element.10) | data formatting | bytes 6144 | tf_op jit(solution)/shard_map/pallas_call | solution.py:263
  121.6 1.4 %copy.7 = f32[4,12,128]{2,0,1:T(4,128)} copy(f32[4,12,128]{2,1,0:T(8,128)} %get-tuple-element.9) | data formatting | bytes 49152 | tf_op jit(solution)/shard_map/pallas_call | solution.py:263
  123.0 0.0 copy-start
  123.0 4.1 %copy.13 = f32[32,24,1024]{2,1,0:T(8,128)} copy(f32[32,24,1024]{2,1,0:T(8,128)} %get-tuple-element.18) | data formatting | bytes 6291456
  127.1 0.0 copy-done
  127.1 0.0 copy-start.1
  127.1 1.1 copy.14
  128.3 0.0 copy-done.1
  128.3 0.7 copy.15
Async XLA Ops:
  123.0 4.1 %copy-start = (f32[16,48,512]{2,1,0:T(8,128)S(1)}, f32[16,48,512]{2,1,0:T(8,128)}, u32[]{:S(2)}) copy-start(f32[16,48,512]{2,1,0:T(8,128)} %get-tuple-element.19) | copy-start | bytes 4718596
  127.1 1.1 copy-start.1

commit v2 on v1

--- a/solution.py
+++ b/solution.py
@@ -131,6 +131,18 @@
             stage.at[target, pl.ds(first, count)], pencil.at[pl.ds(first, count), :, here],
             as_sem.at[target], ar_sem.at[me], (gx, gy, target))
 
+    end = jnp.logical_or(me == 0, me == nz - 1)
+
+    def far(first, count):
+        for d in reversed(range(2, nz)):
+            @pl.when(me + d < nz)
+            def _():
+                block(me + d, first, count).start()
+
+            @pl.when(me - d >= 0)
+            def _():
+                block(me - d, first, count).start()
+
     def near(first):
         @pl.when(me < nz - 1)
         def _():
@@ -139,6 +151,10 @@
         @pl.when(me > 0)
         def _():
             block(me - 1, first, 2).start()
+
+        @pl.when(jnp.logical_not(end))
+        def _():
+            far(first, 2)
 
     def pair(i, carry):
         x = 2 * i
@@ -174,21 +190,9 @@
     def _():
         hop(me, own_one, False).start()
 
-    def far():
-        for d in range(2, nz):
-            @pl.when(me + d < nz)
-            def _():
-                block(me + d, 0, planes).start()
-
-            @pl.when(me - d >= 0)
-            def _():
-                block(me - d, 0, planes).start()
-
-    end = jnp.logical_or(me == 0, me == nz - 1)
-
     @pl.when(end)
     def _():
-        far()
+        far(0, planes)
     keep = pltpu.make_async_copy(
         stage.at[me], pencil.at[:, :, pl.ds(pl.multiple_of(me * depth, LANES), depth)], own_sem.at[0])
     keep.start()
@@ -211,10 +215,6 @@
             @pl.when(me > 0)
             def _():
                 hop(me + k, lanes_of(me + k), False).start()
-        if k == 1:
-            @pl.when(jnp.logical_not(end))
-            def _():
-                far()
     mine.wait()
 
     store = pltpu.make_async_copy(one, one_out, store_sem)
@@ -248,6 +248,29 @@
             remote(stage.at[p], pencil.at[:, :, there], as_sem.at[p], ar_sem.at[p], (gx, gy, p)).wait_recv()
 
 
+def finish(
+    pencil_in, one_in, two_in, three_in, four_in, five_in, pencil, one, two, three, four, five,
+    pencil_buf, one_buf, two_buf, in_sem, out_sem,
+):
+    step = pencil_in.shape[0] // LOADS
+    moves = [
+        (pencil_in.at[pl.ds(k * step, step)], pencil_buf.at[pl.ds(k * step, step)], pencil.at[pl.ds(k * step, step)])
+        for k in range(LOADS)
+    ] + [(one_in, one_buf, one), (two_in, two_buf, two)]
+    loads = [pltpu.make_async_copy(a, b, in_sem.at[i]) for i, (a, b, _) in enumerate(moves)]
+    stores = [pltpu.make_async_copy(b, c, out_sem.at[i]) for i, (_, b, c) in enumerate(moves)]
+    for load in loads:
+        load.start()
+    for source, target in ((three_in, three), (four_in, four), (five_in, five)):
+        for j in range(target.shape[0]):
+            target[j] = source[:, j, :]
+    for load, store in zip(loads, stores):
+        load.wait()
+        store.start()
+    for store in stores:
+        store.wait()
+
+
 def on_device(velocity):
     nx, ny, nz = (lax.axis_size(a) for a in ("gx", "gy", "gz"))
     _, planes, cols, depth = velocity.shape
@@ -260,7 +283,7 @@
     vmem = pl.BlockSpec(memory_space=pltpu.VMEM)
     anywhere = pl.BlockSpec(memory_space=pl.ANY)
     dma = pltpu.SemaphoreType.DMA
-    return pl.pallas_call(
+    first = pl.pallas_call(
         functools.partial(kernel, (nx, ny, nz)),
         out_shape=(jax.ShapeDtypeStruct((planes, cols // nz, full), f32),) + tuple(level(k) for k in range(1, 6)),
         in_specs=[anywhere],
@@ -281,6 +304,15 @@
             collective_id=0, has_side_effects=True, vmem_limit_bytes=60 * 1024 * 1024
         ),
     )(velocity)
+    small = [jax.ShapeDtypeStruct((x.shape[1], x.shape[0], x.shape[2]), f32) for x in first[3:]]
+    last = pl.pallas_call(
+        finish,
+        out_shape=tuple(jax.ShapeDtypeStruct(x.shape, f32) for x in first[:3]) + tuple(small),
+        in_specs=[anywhere] * 3 + [vmem] * 3,
+        out_specs=(anywhere,) * 3 + (vmem,) * 3,
+        scratch_shapes=[pltpu.VMEM(x.shape, f32) for x in first[:3]] + [dma((LOADS + 2,)), dma((LOADS + 2,))],
+    )(*first)
+    return tuple(last[:3]) + tuple(jnp.transpose(x, (1, 0, 2)) for x in last[3:])
 
 
 def solution(mesh):

time: 129 us -> 124 us (0.961)
  local copies, waits for them, and re-layouts: 9.83 us -> 0 us
  Pallas kernels: 118 us -> 123 us
    unnamed x7 -> x0, local copies, waits for them, and re-layouts: 5.91 us -> none
    pallas_call x0 -> x1, Pallas kernels: none -> 5.72 us  [on_device(): pl.pallas_call(finish, out_shape=tuple((jax.ShapeDtypeStruct(x.shape, f32...]
    pallas_call x3 -> x0, local copies, waits for them, and re-layouts: 3.92 us -> none  [on_device(): pl.pallas_call(functools.partial(kernel, (nx, ny, nz)), out_shape=(jax.Sh...]
    pallas_call x1, Pallas kernels: 118 us -> 117 us  [on_device(): pl.pallas_call(functools.partial(kernel, (nx, ny, nz)), out_shape=(jax.Sh...]
where the time goes in v2:
time: 124 us; the launch traced here: 123 us
  Pallas kernels  123 us (99%)
    pallas_call x1, Pallas kernels, on_device(): pl.pallas_call(functools.partial(kernel, (nx, ny, nz)), out_shape=(jax.Sh...  117 us
    pallas_call x1, Pallas kernels, on_device(): pl.pallas_call(finish, out_shape=tuple((jax.ShapeDtypeStruct(x.shape, f32...  5.72 us

profile of v2, /device:TPU:0, one launch (start us, length us, event | category | flops | bytes accessed | tf_op | source)
XLA Modules:
  0.0 123.3 jit_solution(14107381961973897569)
XLA Ops:
  0.6 117.0 %shard_map.62 = (f32[32,24,1024]{2,1,0:T(8,128)}, f32[16,48,512]{2,1,0:T(8,128)}, f32[8,24,256]{2,1,0:T(8,128)}, f32[4,12,128]{2,1,0:T(8,128)}, f32[2,6,64]{2,1,0:T(8,128)}, /*index=5*/f32[1,3,32]{2,1,0:T(4,128)}) custom-call(f32[3,32,96,256]{3,2,1,0:T(8,128)} %vel_hbm.1), custom_call_target="tpu_custom_call" | custom-call | tf_op jit(solution)/shard_map/pallas_call | solution.py:286
  117.6 5.7 %shard_map.63 = (f32[32,24,1024]{2,1,0:T(8,128)}, f32[16,48,512]{2,1,0:T(8,128)}, f32[8,24,256]{2,1,0:T(8,128)}, f32[12,4,128]{2,1,0:T(4,128)}, f32[6,2,64]{2,1,0:T(2,128)}, /*index=5*/f32[3,1,32]{2,1,0:T(1,128)}) custom-call(f32[32,24,1024]{2,1,0:T(8,128)} %get-tuple-element.18.pencil_in, f32[16,48,512]{2,1,0:T(8,128)} %get-tuple-element.19.one_in, ...), custom_call_target="tpu_custom_call" | custom-call | tf_op jit(solution)/shard_map/pallas_call | solution.py:308

commit v3 on v2

--- a/solution.py
+++ b/solution.py
@@ -152,10 +152,6 @@
         def _():
             block(me - 1, first, 2).start()
 
-        @pl.when(jnp.logical_not(end))
-        def _():
-            far(first, 2)
-
     def pair(i, carry):
         x = 2 * i
         summed = None
@@ -215,6 +211,10 @@
             @pl.when(me > 0)
             def _():
                 hop(me + k, lanes_of(me + k), False).start()
+        if k == 1:
+            @pl.when(jnp.logical_not(end))
+            def _():
+                far(0, planes)
     mine.wait()
 
     store = pltpu.make_async_copy(one, one_out, store_sem)

time: 124 us -> 125 us (level)
    pallas_call x1, Pallas kernels: 117 us -> 118 us  [on_device(): pl.pallas_call(functools.partial(kernel, (nx, ny, nz)), out_shape=(jax.Sh...]
where the time goes in v3:
time: 125 us
  Pallas kernels  124 us (99%)
    pallas_call x1, Pallas kernels, on_device(): pl.pallas_call(functools.partial(kernel, (nx, ny, nz)), out_shape=(jax.Sh...  118 us
    pallas_call x1, Pallas kernels, on_device(): pl.pallas_call(finish, out_shape=tuple((jax.ShapeDtypeStruct(x.shape, f32...  5.72 us

profile of v3, /device:TPU:0, one launch (start us, length us, event | category | flops | bytes accessed | tf_op | source)
XLA Modules:
  0.0 124.8 jit_solution(8614463268521433351)
XLA Ops:
  0.6 118.5 %shard_map.62 = (f32[32,24,1024]{2,1,0:T(8,128)}, f32[16,48,512]{2,1,0:T(8,128)}, f32[8,24,256]{2,1,0:T(8,128)}, f32[4,12,128]{2,1,0:T(8,128)}, f32[2,6,64]{2,1,0:T(8,128)}, /*index=5*/f32[1,3,32]{2,1,0:T(4,128)}) custom-call(f32[3,32,96,256]{3,2,1,0:T(8,128)} %vel_hbm.1), custom_call_target="tpu_custom_call" | custom-call | tf_op jit(solution)/shard_map/pallas_call | solution.py:286
  119.1 5.7 %shard_map.63 = (f32[32,24,1024]{2,1,0:T(8,128)}, f32[16,48,512]{2,1,0:T(8,128)}, f32[8,24,256]{2,1,0:T(8,128)}, f32[12,4,128]{2,1,0:T(4,128)}, f32[6,2,64]{2,1,0:T(2,128)}, /*index=5*/f32[3,1,32]{2,1,0:T(1,128)}) custom-call(f32[32,24,1024]{2,1,0:T(8,128)} %get-tuple-element.18.pencil_in, f32[16,48,512]{2,1,0:T(8,128)} %get-tuple-element.19.one_in, ...), custom_call_target="tpu_custom_call" | custom-call | tf_op jit(solution)/shard_map/pallas_call | solution.py:308
